TPU v7x, 32 devices: a whole 2x2x4 slice. The times are simulated.
32 devices in a mesh: dp: 4 (over z), mp: 8 (over y, x, core).
Axes of the slice: x: 2, y: 2, z: 4, core: 2. Of those that a mesh axis runs over, the one named last changes fastest.
Arguments:
- tokens: bfloat16 [4096, 4096], P('dp', 'mp'), may hold values from -6 to 6
- decay: float32 [4096, 16], P('dp'), may hold values from 0.75 to 1, as said below
- state: float32 [128, 256, 8192], P('dp', None, 'mp'), may hold values from -24 to 24
- w_query: bfloat16 [4096, 4096], P(None, 'mp'), may hold values from -0.09375 to 0.09375
- w_key: bfloat16 [4096, 4096], P(None, 'mp'), may hold values from -0.09375 to 0.09375
- w_value: bfloat16 [4096, 8192], P(None, 'mp'), may hold values from -0.09375 to 0.09375
- w_gate: bfloat16 [4096, 8192], P(None, 'mp'), may hold values from -0.09375 to 0.09375
- w_out: bfloat16 [8192, 4096], P('mp'), may hold values from -0.09375 to 0.09375
- norm_gain: float32 [8192], P('mp'), may hold values from 0.25 to 1.75
Outputs:
- layer_out: bfloat16 [4096, 4096], P('dp', 'mp')
- new_state: float32 [128, 256, 8192], P('dp', None, 'mp')
Inputs may be any that keep to these rules, and one draw needn't show every extreme that they name: `decay`: each head has its own base rate over all tokens, varied somewhat from token to token.
All inputs are finite; a program needn't handle non-finite values.
Results may differ from a plain program's by a relative error of at most 0.0071.
Values may be sent and summed in bfloat16 or wider, within the bound.
A program may use at most 256 MiB of HBM per device.

v0:
```python
import jax
import jax.numpy as jnp
from jax import lax
from jax.sharding import PartitionSpec as P

HEAD = 256
VHEAD = 512
NEW = 32
EPS = 0.1


def partner(shard, axis, bit):
    return lax.ppermute(shard, axis, [(i, i ^ 1 << bit) for i in range(lax.axis_size(axis))])


def per_device(tokens, decay, state, w_query, w_key, w_value, w_gate, w_out, norm_gain):
    highest = lax.Precision.HIGHEST
    tok_rows = tokens.shape[0]
    qk_columns = w_query.shape[1]
    v_columns = w_value.shape[1]
    head_span = max(1, HEAD // qk_columns)
    groups = max(1, qk_columns // HEAD)
    qk_width = qk_columns // groups
    v_width = v_columns // groups
    sequences = tok_rows // NEW
    bit_count = head_span.bit_length() - 1
    device_index = lax.axis_index("mp")
    first_head = device_index * qk_columns // HEAD
    qk_zeros = jnp.zeros((tok_rows, qk_columns), jnp.float32)
    v_zeros = jnp.zeros((tok_rows, v_columns), jnp.float32)
    carried = (qk_zeros, qk_zeros, v_zeros, v_zeros)
    segment = lax.all_gather(tokens, "mp", axis=1, tiled=True)
    updated = []
    for running, weight in zip(carried, (w_query, w_key, w_value, w_gate)):
        updated.append(jnp.dot(segment, weight, preferred_element_type=jnp.float32))
    query, key_proj, value_proj, gate_proj = tuple(updated)
    query = (query * HEAD ** (-0.5)).astype(jnp.bfloat16).reshape(tok_rows, groups, qk_width)
    key_proj = key_proj.astype(jnp.bfloat16).reshape(tok_rows, groups, qk_width)
    value_proj = value_proj.astype(jnp.bfloat16)
    for bit_number in range(bit_count):
        other_query, other_key = partner((query, key_proj), "mp", bit_number)
        upper_half = device_index >> bit_number & 1 == 1
        query = jnp.where(
            upper_half,
            jnp.concatenate([other_query, query], 2),
            jnp.concatenate([query, other_query], 2),
        )
        key_proj = jnp.where(
            upper_half,
            jnp.concatenate([other_key, key_proj], 2),
            jnp.concatenate([key_proj, other_key], 2),
        )
    query_block = query.reshape(sequences, NEW, groups, HEAD)
    key_block = key_proj.reshape(sequences, NEW, groups, HEAD)
    value_block = value_proj.reshape(sequences, NEW, groups, v_width)
    decay_rates = lax.dynamic_slice_in_dim(decay, first_head, groups, 1).reshape(
        sequences, NEW, groups
    )
    log_cumul = jnp.cumsum(jnp.log(decay_rates), axis=1)
    old_state = state.reshape(sequences, HEAD, groups, v_width)
    from_state = jnp.einsum(
        "bngk,bkgv->bngv", query_block.astype(jnp.float32), old_state, precision=highest
    )
    scores = jnp.einsum(
        "bngk,bmgk->bgnm", query_block, key_block, preferred_element_type=jnp.float32
    )
    along = jnp.transpose(log_cumul, (0, 2, 1))
    log_gap = along[:, :, :, None] - along[:, :, None, :]
    causal = jnp.arange(NEW)[:, None] >= jnp.arange(NEW)[None, :]
    factor = jnp.where(causal, jnp.exp(jnp.where(causal, log_gap, 0.0)), 0.0)
    weights = (scores * factor).astype(jnp.bfloat16)
    in_block = jnp.einsum(
        "bgnm,bmgv->bngv", weights, value_block, preferred_element_type=jnp.float32
    )
    retained = jnp.exp(log_cumul)[..., None] * from_state + in_block
    final_log = log_cumul[:, -1, :]
    carry_scale = jnp.exp(final_log[:, None, :] - log_cumul)
    decayed_keys = key_block.astype(jnp.float32) * carry_scale[..., None]
    fresh = jnp.einsum(
        "bngk,bngv->bkgv", decayed_keys, value_block.astype(jnp.float32), precision=highest
    )
    new_state = jnp.exp(final_log)[:, None, :, None] * old_state + fresh
    new_state = new_state.reshape(sequences, HEAD, v_columns)
    retained = retained.reshape(tok_rows, groups, v_width)
    running = jnp.sum(retained, axis=-1)
    squares = jnp.sum(retained * retained, axis=-1)
    for bit_number in range(bit_count):
        other_sum, other_square = partner((running, squares), "mp", bit_number)
        running = running + other_sum
        squares = squares + other_square
    centre = running / VHEAD
    variance = squares / VHEAD - centre * centre
    deviation = retained - centre[..., None]
    normed = deviation * lax.rsqrt(variance + EPS)[..., None]
    gated_out = (normed.reshape(tok_rows, v_columns) * norm_gain * jax.nn.silu(gate_proj)).astype(
        jnp.bfloat16
    )
    partial_terms = jnp.dot(gated_out, w_out, preferred_element_type=jnp.float32)
    layer_out = lax.psum_scatter(partial_terms, "mp", scatter_dimension=1, tiled=True).astype(
        jnp.bfloat16
    )
    return (layer_out, new_state)


def solution(mesh):
    placed = (
        P("dp", "mp"),
        P("dp", None),
        P("dp", None, "mp"),
        P(None, "mp"),
        P(None, "mp"),
        P(None, "mp"),
        P(None, "mp"),
        P("mp", None),
        P("mp"),
    )
    return jax.shard_map(
        per_device,
        mesh=mesh,
        in_specs=placed,
        out_specs=(P("dp", "mp"), P("dp", None, "mp")),
        check_vma=False,
    )
```

profile of v0, /device:TPU:0, one launch (start us, length us, event | category | flops | bytes accessed | tf_op | source)
XLA Modules:
  0.0 312.2 jit_solution(14913403613981106068)
XLA Ops:
  7.2 0.0 all-gather.2.cloned.1.call-start
  7.2 0.7 all-gather.2.cloned.1.call-update
  7.9 0.0 reduce-scatter.2.cloned.1.call-start
  8.0 0.9 dynamic-slice_log_fusion
  8.8 0.1 log.7
  8.9 0.5 copy.82
  9.5 2.0 fusion.33
  11.5 0.4 copy.89
  11.8 33.6 %copy.84 = f32[32,256,1024]{1,2,0:T(8,128)} copy(f32[32,256,1024]{2,1,0:T(8,128)} %param.11) | data formatting | bytes 67108864 | tf_op args[2]
  45.5 0.1 copy.97
  45.6 0.6 copy-done.2
  46.1 0.1 copy.100
  46.2 0.9 subtract_exponential_fusion
  47.2 0.4 copy.83
  47.5 20.9 %all-gather.2.cloned.1.call-done = bf16[1024,4096]{1,0:T(8,128)(2,1)} async-done(((bf16[1024,512]{1,0:T(8,128)(2,1)}), bf16[1024,4096]{1,0:T(8,128)(2,1)}) %all-gather.2.cloned.1.call-update) | async-done | bytes 8388624 | tf_op jit(solution)/shard_map/all_gather | solution.py:32
  68.5 14.7 %convolution_convert_fusion = bf16[1024,1024]{1,0:T(8,128)(2,1)} fusion(bf16[1024,4096]{1,0:T(8,128)(2,1)} %all-gather.2.cloned.1.call-done, bf16[4096,1024]{1,0:T(8,128)(2,1)} %param.14), kind=kOutput, calls=%fused_computation.11 | convolution fusion | flops 8590983168 | bytes 18874368 | tf_op jit(solution)/shard_map/dot_general | solution.py:35
  83.1 3.3 %reshape.64 = bf16[32,32,2,512]{3,2,1,0:T(2,128)(2,1)S(1)} reshape(bf16[1024,1024]{1,0:T(8,128)(2,1)} %convolution_convert_fusion) | data formatting | bytes 4194304 | tf_op jit(solution)/shard_map/reshape | solution.py:55
  86.5 10.0 %convolution_convert_fusion.1 = bf16[1024,512]{1,0:T(8,128)(2,1)} fusion(bf16[1024,4096]{1,0:T(8,128)(2,1)} %all-gather.2.cloned.1.call-done, bf16[4096,512]{1,0:T(8,128)(2,1)} %param.13), kind=kOutput, calls=%fused_computation.14 | convolution fusion | flops 4295491584 | bytes 13631488 | tf_op jit(solution)/shard_map/dot_general | solution.py:35
  96.5 1.3 reshape_reshape.7
  97.8 10.0 %multiply_convert_fusion.2 = bf16[1024,512]{1,0:T(8,128)(2,1)} fusion(bf16[1024,4096]{1,0:T(8,128)(2,1)} %all-gather.2.cloned.1.call-done, bf16[4096,512]{1,0:T(8,128)(2,1)} %param.12), kind=kOutput, calls=%fused_computation.10 | convolution fusion | flops 4296015872 | bytes 13631488 | tf_op jit(solution)/shard_map/dot_general | solution.py:35
  107.9 2.2 reshape_reshape.6
  110.1 21.4 %fusion.18 = f32[32,2,32,512]{3,2,1,0:T(8,128)} fusion(f32[32,256,2,512]{1,3,2,0:T(8,128)} %bitcast.37, bf16[32,32,2,256]{3,2,1,0:T(2,128)(2,1)} %reshape_reshape.6), kind=kOutput, calls=%fused_computation.25 | convolution fusion | flops 3221225472 | bytes 38797312 | tf_op jit(solution)/shard_map/bngk,bkgv->bngv/dot_general | solution.py:61
  131.5 4.9 %fusion.26 = (f32[32,32,2]{1,2,0:T(2,128)S(1)}, f32[32,32,2]{1,2,0:T(2,128)S(1)}, f32[32,32,2,512]{3,1,2,0:T(8,128)}) fusion(bf16[32,32,2,512]{3,2,1,0:T(2,128)(2,1)S(1)} %reshape.64, bf16[32,32,2,256]{3,2,1,0:T(2,128)(2,1)S(1)} %reshape_reshape.7, bf16[32,32,2,256]{3,2,1,0:T(2,128)(2,1)} %reshape_reshape.6, f32[32,2,32]{2,1,0:T(2,128)S(1)} %copy.89, ...), kind=kOutput, calls=%fused_computation.40 | convolution fusion | flops 106229760 | bytes 12616704 | tf_op jit(solution)/shard_map/bgnm,bmgv->bngv/dot_general | solution.py:72
  136.4 0.1 div.28
  136.5 0.1 div.26
  136.6 1.0 copy.94
  137.7 1.0 copy.96
  138.7 2.9 mul.81
  141.6 0.0 copy-start
  141.6 3.0 copy.107
  144.6 0.0 copy-done
  144.6 3.3 %copy.92 = f32[32,32,2,512]{3,2,1,0:T(2,128)S(1)} copy(f32[32,32,2,512]{3,1,2,0:T(8,128)S(1)} %copy-done) | data formatting | bytes 8388608 | tf_op jit(solution)/shard_map/add | solution.py:75
  147.9 0.0 copy-start.1
  147.9 3.0 copy.105
  150.9 0.0 copy-done.1
  150.9 1.4 sub.51
  152.3 0.0 copy-start.4
  152.3 2.9 copy.106
  155.2 0.0 copy-done.4
  155.2 31.2 %fusion = f32[1024,4096]{1,0:T(8,128)} fusion(bf16[1024,4096]{1,0:T(8,128)(2,1)} %param.16, f32[1024,1024]{1,0:T(8,128)} %bitcast.44, f32[1024,1024]{1,0:T(8,128)} %bitcast.45, f32[1024,1024]{1,0:T(8,128)} %bitcast.46, f32[1024]{0:T(1024)S(1)} %copy-done.4, bf16[1024,4096]{1,0:T(8,128)(2,1)} %all-gather.2.cloned.1.call-done, bf16[4096,1024]{1,0:T(8,128)(2,1)} %param.15), kind=kOutput, calls=%fused_computation.5 | convolution fusion | flops 17189306368 | bytes 54530048 | tf_op jit(solution)/shard_map/dot_general | solution.py:98
  186.5 0.0 reduce-scatter.2.cloned.1.call-update
  186.5 0.6 copy-done.3
  187.2 0.1 copy.98
  187.2 1.4 copy.101
  188.6 28.9 %bitcast_add_fusion = f32[32,256,2,512]{1,3,2,0:T(8,128)} fusion(f32[32,256,2,512]{1,3,2,0:T(8,128)} %bitcast.38, f32[32,2]{1,0:T(8,128)S(1)} %copy.98, bf16[32,32,2,512]{3,2,1,0:T(2,128)(2,1)S(1)} %reshape.64, f32[32,32,2]{1,2,0:T(2,128)S(1)} %copy.101, bf16[32,32,2,256]{3,2,1,0:T(2,128)(2,1)S(1)} %reshape_reshape.7), kind=kOutput, calls=%fused_computation | convolution fusion | flops 3239051264 | bytes 70263040 | tf_op jit(solution)/shard_map/bngk,bngv->bkgv/dot_general | solution.py:79
  217.5 33.7 %copy.103 = f32[32,256,1024]{2,1,0:T(8,128)} copy(f32[32,256,1024]{1,2,0:T(8,128)} %bitcast.39) | data formatting | bytes 67108864
  251.3 51.4 %reduce-scatter.2.cloned.1.call-done = f32[1024,512]{1,0:T(8,128)} async-done(((f32[1024,4096]{1,0:T(8,128)}), f32[1024,512]{1,0:T(8,128)}) %reduce-scatter.2.cloned.1.call-update) | async-done | bytes 2097168 | tf_op jit(solution)/shard_map/reduce_scatter | solution.py:99
  302.7 2.7 convert_element_type.28
  (7 shorter events, 0.0 us)
Async XLA Ops:
  7.2 61.3 %all-gather.2.cloned.1.call-start = ((), (), s32[]{:S(2)}) async-start(), calls=%async_computation.1 | async-start | bytes 9437184 | tf_op jit(solution)/shard_map/all_gather | solution.py:32
  7.9 294.8 %reduce-scatter.2.cloned.1.call-start = ((), (), s32[]{:S(2)}) async-start(), calls=%async_computation.2 | async-start | bytes 18874368 | tf_op jit(solution)/shard_map/reduce_scatter | solution.py:99
  45.6 0.6 copy-start.2
  141.6 3.0 copy-start
  147.9 3.0 copy-start.1
  152.3 3.0 copy-start.4
  186.5 0.7 copy-start.3
Sparse Core Ops, SparseCore 0:
  9.8 58.5 all-gather.1
  186.6 115.9 reduce-scatter.1
where the time goes:
time: 314 us; the launch traced here: 312 us
  matrix products  121 us (39%)
  local copies, waits for them, and re-layouts  98 us (31%)
  waiting for transfers between devices  73 us (23%)
  between operations  14.2 us (5%)
  other arithmetic  5.65 us (2%)
    unnamed x15, local copies, waits for them, and re-layouts  77.5 us
    reduce_scatter x1, waiting for transfers between devices, per_device(): lax.psum_scatter(partial_terms, 'mp', scatter_dimension=1, tiled=True)  51.4 us
    dot_general x3, matrix products, per_device(): updated.append(jnp.dot(segment, weight, preferred_element_type=jnp.float32))  34.7 us
    dot_general x1, matrix products, per_device(): jnp.dot(gated_out, w_out, preferred_element_type=jnp.float32)  31.2 us
    dot_general x1, matrix products, per_device(): jnp.einsum('bngk,bngv->bkgv', decayed_keys, value_block.astype(jnp.float3...  28.9 us
    dot_general x1, matrix products, per_device(): jnp.einsum('bngk,bkgv->bngv', query_block.astype(jnp.float32), old_state,...  21.4 us
    all_gather x1, waiting for transfers between devices, per_device(): segment = lax.all_gather(tokens, 'mp', axis=1, tiled=True)  20.9 us
  transfers between devices with their start and end apart: 2, of which 2 were waited for; matrix products, arithmetic and copies ran while one was open for 33% of the time, Pallas kernels for 0%

commit v1 on v0

--- a/solution.py
+++ b/solution.py
@@ -29,7 +29,7 @@
     qk_zeros = jnp.zeros((tok_rows, qk_columns), jnp.float32)
     v_zeros = jnp.zeros((tok_rows, v_columns), jnp.float32)
     carried = (qk_zeros, qk_zeros, v_zeros, v_zeros)
-    segment = lax.all_gather(tokens, "mp", axis=1, tiled=True)
+    segment = jnp.concatenate(lax.all_gather(tokens, "mp"), axis=1)
     updated = []
     for running, weight in zip(carried, (w_query, w_key, w_value, w_gate)):
         updated.append(jnp.dot(segment, weight, preferred_element_type=jnp.float32))

time: 314 us -> 324 us (1.032)
  local copies, waits for them, and re-layouts: 98 us -> 110 us
    reshape x0 -> x1, local copies, waits for them, and re-layouts: none -> 11.5 us  [per_device(): segment = jnp.concatenate(lax.all_gather(tokens, 'mp'), axis=1)]
  transfers between devices with their start and end apart: 2 -> 2, of which waited for: 2 -> 2; matrix products, arithmetic and copies ran while one was open for 33% -> 32% of each run, Pallas kernels for 0% -> 0%
where the time goes in v1:
time: 324 us; the launch traced here: 323 us
  matrix products  122 us (38%)
  local copies, waits for them, and re-layouts  110 us (34%)
  waiting for transfers between devices  71.5 us (22%)
  between operations  14.2 us (4%)
  other arithmetic  5.65 us (2%)
    unnamed x15, local copies, waits for them, and re-layouts  77.4 us
    reduce_scatter x1, waiting for transfers between devices, per_device(): lax.psum_scatter(partial_terms, 'mp', scatter_dimension=1, tiled=True)  51.4 us
    dot_general x3, matrix products, per_device(): updated.append(jnp.dot(segment, weight, preferred_element_type=jnp.float32))  34.9 us
    dot_general x1, matrix products, per_device(): jnp.dot(gated_out, w_out, preferred_element_type=jnp.float32)  31.4 us
    dot_general x1, matrix products, per_device(): jnp.einsum('bngk,bngv->bkgv', decayed_keys, value_block.astype(jnp.float3...  28.9 us
    dot_general x1, matrix products, per_device(): jnp.einsum('bngk,bkgv->bngv', query_block.astype(jnp.float32), old_state,...  21.5 us
    all_gather x1, waiting for transfers between devices, per_device(): segment = jnp.concatenate(lax.all_gather(tokens, 'mp'), axis=1)  19.4 us
    reshape x1, local copies, waits for them, and re-layouts, per_device(): segment = jnp.concatenate(lax.all_gather(tokens, 'mp'), axis=1)  11.5 us
  transfers between devices with their start and end apart: 2, of which 2 were waited for; matrix products, arithmetic and copies ran while one was open for 32% of the time, Pallas kernels for 0%

profile of v1, /device:TPU:0, one launch (start us, length us, event | category | flops | bytes accessed | tf_op | source)
XLA Modules:
  0.0 322.8 jit_solution(16683079162742021138)
XLA Ops:
  7.2 0.0 all-gather.3.cloned.1.call-start
  7.2 0.7 all-gather.3.cloned.1.call-update
  7.9 0.0 reduce-scatter.2.cloned.1.call-start
  8.0 0.9 dynamic-slice_log_fusion
  8.8 0.1 log.7
  8.9 0.5 copy.103
  9.5 2.0 fusion.33
  11.5 0.4 copy.111
  11.8 33.6 %copy.106 = f32[32,256,1024]{1,2,0:T(8,128)} copy(f32[32,256,1024]{2,1,0:T(8,128)} %param.11) | data formatting | bytes 67108864 | tf_op args[2]
  45.5 0.1 copy.119
  45.5 0.6 copy-done.3
  46.1 0.1 copy.122
  46.2 0.9 subtract_exponential_fusion
  47.1 0.4 copy.104
  47.5 19.4 %all-gather.3.cloned.1.call-done = bf16[8192,512]{1,0:T(8,128)(2,1)} async-done(((bf16[1024,512]{1,0:T(8,128)(2,1)}), bf16[8192,512]{1,0:T(8,128)(2,1)}) %all-gather.3.cloned.1.call-update) | async-done | bytes 8388624 | tf_op jit(solution)/shard_map/all_gather | solution.py:32
  66.9 11.5 %copy.105 = bf16[1024,8,512]{0,2,1:T(8,128)(2,1)} copy(bf16[1024,8,512]{2,0,1:T(8,128)(2,1)} %bitcast.54) | data formatting | bytes 16777216 | tf_op jit(solution)/shard_map/reshape | solution.py:32
  78.4 14.7 %convolution_convert_fusion = bf16[1024,1024]{1,0:T(8,128)(2,1)} fusion(bf16[1024,4096]{0,1:T(8,128)(2,1)} %bitcast.44, bf16[4096,1024]{1,0:T(8,128)(2,1)} %param.14), kind=kOutput, calls=%fused_computation.11 | convolution fusion | flops 8590983168 | bytes 18874368 | tf_op jit(solution)/shard_map/dot_general | solution.py:35
  93.1 3.3 %reshape.72 = bf16[32,32,2,512]{3,2,1,0:T(2,128)(2,1)S(1)} reshape(bf16[1024,1024]{1,0:T(8,128)(2,1)} %convolution_convert_fusion) | data formatting | bytes 4194304 | tf_op jit(solution)/shard_map/reshape | solution.py:55
  96.4 10.1 %convolution_convert_fusion.1 = bf16[1024,512]{1,0:T(8,128)(2,1)} fusion(bf16[1024,4096]{0,1:T(8,128)(2,1)} %bitcast.45, bf16[4096,512]{1,0:T(8,128)(2,1)} %param.13), kind=kOutput, calls=%fused_computation.14 | convolution fusion | flops 4295491584 | bytes 13631488 | tf_op jit(solution)/shard_map/dot_general | solution.py:35
  106.5 1.5 reshape_reshape.7
  108.0 10.1 %multiply_convert_fusion.2 = bf16[1024,512]{1,0:T(8,128)(2,1)} fusion(bf16[1024,4096]{0,1:T(8,128)(2,1)} %bitcast.46, bf16[4096,512]{1,0:T(8,128)(2,1)} %param.12), kind=kOutput, calls=%fused_computation.10 | convolution fusion | flops 4296015872 | bytes 13631488 | tf_op jit(solution)/shard_map/dot_general | solution.py:35
  118.1 2.2 reshape_reshape.6
  120.3 21.5 %fusion.18 = f32[32,2,32,512]{3,2,1,0:T(8,128)} fusion(f32[32,256,2,512]{1,3,2,0:T(8,128)} %bitcast.41, bf16[32,32,2,256]{3,2,1,0:T(2,128)(2,1)} %reshape_reshape.6), kind=kOutput, calls=%fused_computation.25 | convolution fusion | flops 3221225472 | bytes 38797312 | tf_op jit(solution)/shard_map/bngk,bkgv->bngv/dot_general | solution.py:61
  141.8 4.9 %fusion.26 = (f32[32,32,2]{1,2,0:T(2,128)S(1)}, f32[32,32,2]{1,2,0:T(2,128)S(1)}, f32[32,32,2,512]{3,1,2,0:T(8,128)}) fusion(bf16[32,32,2,512]{3,2,1,0:T(2,128)(2,1)S(1)} %reshape.72, bf16[32,32,2,256]{3,2,1,0:T(2,128)(2,1)S(1)} %reshape_reshape.7, bf16[32,32,2,256]{3,2,1,0:T(2,128)(2,1)} %reshape_reshape.6, f32[32,2,32]{2,1,0:T(2,128)S(1)} %copy.111, ...), kind=kOutput, calls=%fused_computation.40 | convolution fusion | flops 106229760 | bytes 12616704 | tf_op jit(solution)/shard_map/bgnm,bmgv->bngv/dot_general | solution.py:72
  146.7 0.1 div.28
  146.8 0.1 div.26
  146.8 1.0 copy.116
  147.9 1.0 copy.118
  148.9 3.1 mul.81
  152.0 0.0 copy-start.1
  152.0 3.0 copy.129
  155.0 0.0 copy-done.1
  155.0 3.3 %copy.114 = f32[32,32,2,512]{3,2,1,0:T(2,128)S(1)} copy(f32[32,32,2,512]{3,1,2,0:T(8,128)S(1)} %copy-done.1) | data formatting | bytes 8388608 | tf_op jit(solution)/shard_map/add | solution.py:75
  158.4 0.0 copy-start.2
  158.4 3.0 copy.127
  161.3 1.4 sub.51
  162.7 0.0 copy-start
  162.7 2.9 copy.128
  165.7 0.0 copy-done
  165.7 31.4 %fusion = f32[1024,4096]{1,0:T(8,128)} fusion(bf16[1024,4096]{1,0:T(8,128)(2,1)} %param.16, f32[1024,1024]{1,0:T(8,128)} %bitcast.48, f32[1024,1024]{1,0:T(8,128)} %bitcast.49, f32[1024,1024]{1,0:T(8,128)} %bitcast.50, f32[1024]{0:T(1024)S(1)} %copy-done, bf16[1024,4096]{0,1:T(8,128)(2,1)} %bitcast.47, bf16[4096,1024]{1,0:T(8,128)(2,1)} %param.15), kind=kOutput, calls=%fused_computation.5 | convolution fusion | flops 17189306368 | bytes 54530048 | tf_op jit(solution)/shard_map/dot_general | solution.py:98
  197.1 0.0 reduce-scatter.2.cloned.1.call-update
  197.1 0.6 copy-done.4
  197.8 0.1 copy.120
  197.8 1.4 copy.123
  199.2 28.9 %bitcast_add_fusion = f32[32,256,2,512]{1,3,2,0:T(8,128)} fusion(f32[32,256,2,512]{1,3,2,0:T(8,128)} %bitcast.42, f32[32,2]{1,0:T(8,128)S(1)} %copy.120, bf16[32,32,2,512]{3,2,1,0:T(2,128)(2,1)S(1)} %reshape.72, f32[32,32,2]{1,2,0:T(2,128)S(1)} %copy.123, bf16[32,32,2,256]{3,2,1,0:T(2,128)(2,1)S(1)} %reshape_reshape.7), kind=kOutput, calls=%fused_computation | convolution fusion | flops 3239051264 | bytes 70263040 | tf_op jit(solution)/shard_map/bngk,bngv->bkgv/dot_general | solution.py:79
  228.1 33.7 %copy.125 = f32[32,256,1024]{2,1,0:T(8,128)} copy(f32[32,256,1024]{1,2,0:T(8,128)} %bitcast.43) | data formatting | bytes 67108864
  261.8 51.4 %reduce-scatter.2.cloned.1.call-done = f32[1024,512]{1,0:T(8,128)} async-done(((f32[1024,4096]{1,0:T(8,128)}), f32[1024,512]{1,0:T(8,128)}) %reduce-scatter.2.cloned.1.call-update) | async-done | bytes 2097168 | tf_op jit(solution)/shard_map/reduce_scatter | solution.py:99
  313.3 2.7 convert_element_type.28
  (8 shorter events, 0.0 us)
Async XLA Ops:
  7.2 59.7 %all-gather.3.cloned.1.call-start = ((), (), s32[]{:S(2)}) async-start(), calls=%async_computation.2 | async-start | bytes 9437184 | tf_op jit(solution)/shard_map/all_gather | solution.py:32
  7.9 305.4 %reduce-scatter.2.cloned.1.call-start = ((), (), s32[]{:S(2)}) async-start(), calls=%async_computation.1 | async-start | bytes 18874368 | tf_op jit(solution)/shard_map/reduce_scatter | solution.py:99
  45.5 0.6 copy-start.3
  152.0 3.0 copy-start.1
  158.4 3.0 copy-start.2
  162.7 3.0 copy-start
  197.1 0.7 copy-start.4
Sparse Core Ops, SparseCore 0:
  9.9 56.9 all-gather.2
  197.2 115.9 reduce-scatter.1
